TPU v7x, 32 devices: a whole 2x2x4 slice. The times are simulated.
32 devices in a mesh: sub: 16 (over z, y, x), crs: 2 (over core).
Axes of the slice: x: 2, y: 2, z: 4, core: 2. Of those that a mesh axis runs over, the one named last changes fastest.
Arguments:
- multipliers: float32 [16, 128, 512], P(None, ('sub', 'crs')), may hold values from -6 to 6
- own_modes: float32 [6, 128, 512], P(None, ('sub', 'crs')), may hold values from -0.75 to 0.75
- neighbour_modes: float32 [6, 128, 512], P(None, ('sub', 'crs')), may hold values from -0.75 to 0.75
- face_index: int32 [128, 512], P(('sub', 'crs')), may hold values from 0 to 5, as said below
- neighbour_list: int32 [128, 6], replicated, may hold values from 0 to 127, as said below
- coarse_factor: float32 [768, 768], P('sub', 'crs'), may hold values from -0.21875 to 0.21875
Outputs:
- projected: float32 [16, 128, 512], P(None, ('sub', 'crs'))
Inputs may be any that keep to these rules, and one draw needn't show every extreme that they name: `face_index`: the multipliers of each subdomain lie in 6 contiguous nonempty blocks, face 0 first and face 5 last. `neighbour_list`: subdomain s = (8 x + y) * 8 + z sits at (x, y, z) of a periodic grid of 2 x 8 x 8 subdomains; the 6 faces of each subdomain name its grid neighbours x plus 1, x minus 1, y plus or minus 1, z plus or minus 1 (periodic; along the first dimension both name the same subdomain), in an order that differs from subdomain to subdomain.
All inputs are finite; a program needn't handle non-finite values.
Results may differ from a plain program's by a relative error of at most 0.0001.
Values sent between devices are 32-bit elements; how exact they have to be, the bound alone decides.
No kernel may reach another device: no remote copies, remote signals or barrier semaphores. Data moves between devices by JAX's collectives and lax.ppermute only.
A program may use at most 64 MiB of HBM per device.

v0:
```python
import jax
import jax.numpy as jnp
from jax import lax
from jax.sharding import PartitionSpec as P

MODES = 6
NFACE = 6


HIGHEST = lax.Precision.HIGHEST


def shifted(value, axis, by):
    peers = lax.axis_size(axis)
    return lax.ppermute(value, axis, [(i, (i + by) % peers) for i in range(peers)])


def select_columns(portion, positions, wanted):
    matches = (positions[:, None] == wanted[None, :]).astype(jnp.float32)
    return jnp.einsum("krn,nt->krt", portion, matches, precision=HIGHEST)


def body(multipliers, own_modes, neighbour_modes, face_index, neighbour_list, coarse_factor):
    width_rhs = multipliers.shape[0]
    local_subs = multipliers.shape[1]
    crs_size = lax.axis_size("crs")
    sub_size = lax.axis_size("sub")
    crs_rank = lax.axis_index("crs")
    sub_rank = lax.axis_index("sub")
    group_subs = local_subs * crs_size
    faces_dev = local_subs * NFACE
    first_sub = (sub_rank * crs_size + crs_rank) * local_subs
    flat_targets = neighbour_list.reshape(-1)
    row_len = sub_size // 2
    col_len = sub_size // row_len
    row_place = sub_rank % row_len
    local_ids = first_sub + lax.iota(jnp.int32, local_subs)
    first = local_ids // (row_len * group_subs)
    second = local_ids // group_subs % row_len
    third = local_ids % group_subs

    def place(a, b, c):
        return (a * row_len + b) * group_subs + c

    grid_next = jnp.stack(
        [
            place((first + 1) % col_len, second, third),
            place((first + col_len - 1) % col_len, second, third),
            place(first, (second + 1) % row_len, third),
            place(first, (second + row_len - 1) % row_len, third),
            place(first, second, (third + 1) % group_subs),
            place(first, second, (third + group_subs - 1) % group_subs),
        ],
        axis=1,
    )
    local_nbrs = lax.dynamic_slice_in_dim(neighbour_list, first_sub, local_subs, 0)
    matches = (local_nbrs[:, :, None] == grid_next[:, None, :]).astype(jnp.int32)
    first_hit = matches * (jnp.cumsum(matches, axis=2) == 1).astype(jnp.int32)
    face_dir = first_hit.astype(jnp.float32)
    masked_modes = []
    for which_face in range(NFACE):
        masked_modes.append(neighbour_modes * (face_index == which_face).astype(jnp.float32)[None])
    own_coarse = jnp.einsum("ksm,rsm->krs", own_modes, multipliers, precision=HIGHEST)
    face_parts = []
    for which_face in range(NFACE):
        face_parts.append(
            jnp.einsum("ksm,rsm->krs", masked_modes[which_face], multipliers, precision=HIGHEST)
        )
    face_stack = jnp.stack(face_parts, axis=3)
    outgoing = jnp.einsum("krjf,jfd->dkrj", face_stack, face_dir, precision=HIGHEST)
    plans = [(0, row_len), (1, -row_len), (2, 1), (2, 1 - row_len), (3, -1), (3, row_len - 1)]
    arrived = []
    for direction, step in plans:
        arrived.append(shifted(outgoing[direction], "sub", step))
    plus_y = jnp.where(row_place == 0, arrived[3], arrived[2])
    minus_y = jnp.where(row_place == row_len - 1, arrived[5], arrived[4])
    upward = outgoing[4]
    downward = outgoing[5]
    crossing = []
    for piece, step in ((upward[:, :, -1:], 1), (downward[:, :, :1], -1)):
        crossing.append(shifted(piece, "crs", step))
    from_below = jnp.concatenate([crossing[0], upward[:, :, :-1]], axis=2)
    from_above = jnp.concatenate([downward[:, :, 1:], crossing[1]], axis=2)
    own_total = own_coarse + arrived[0] + arrived[1] + plus_y + minus_y + from_below + from_above
    group_coarse = lax.all_gather(own_total, "crs", axis=2, tiled=True)
    coarse_rhs = group_coarse.transpose(2, 0, 1).reshape(group_subs * MODES, width_rhs)
    partial_rows = jnp.einsum("cp,cr->pr", coarse_factor, coarse_rhs, precision=HIGHEST)
    panel_rows = lax.psum(partial_rows, "sub")
    partial_modes = jnp.dot(
        coarse_factor, panel_rows, precision=HIGHEST, preferred_element_type=jnp.float32
    )
    partial_modes = partial_modes.reshape(group_subs, MODES, width_rhs).transpose(1, 2, 0)
    local_targets = lax.dynamic_slice_in_dim(flat_targets, first_sub * NFACE, faces_dev)
    group_amps = lax.psum(partial_modes, "crs")
    own_amps = lax.dynamic_slice_in_dim(group_amps, crs_rank * local_subs, local_subs, 2)
    portion = lax.all_gather(group_amps, "sub", axis=2, tiled=True)
    positions = lax.iota(jnp.int32, portion.shape[2])
    near_amps = select_columns(portion, positions, local_targets)
    near_amps = near_amps.reshape(MODES, width_rhs, local_subs, NFACE)
    applied = jnp.einsum("ksm,krs->rsm", own_modes, own_amps, precision=HIGHEST)
    for which_face in range(NFACE):
        applied = applied + jnp.einsum(
            "ksm,krs->rsm",
            masked_modes[which_face],
            near_amps[:, :, :, which_face],
            precision=HIGHEST,
        )
    return multipliers - applied


def solution(mesh):
    placed = (
        P(None, ("sub", "crs"), None),
        P(None, ("sub", "crs"), None),
        P(None, ("sub", "crs"), None),
        P(("sub", "crs"), None),
        P(),
        P("sub", "crs"),
    )
    return jax.shard_map(
        body, mesh=mesh, in_specs=placed, out_specs=P(None, ("sub", "crs"), None), check_vma=False
    )
```

profile of v0, /device:TPU:0, one launch (start us, length us, event | category | flops | bytes accessed | tf_op | source)
XLA Modules:
  0.0 146.9 jit_solution(12411067293623808287)
XLA Ops:
  0.0 0.0 copy-start
  0.0 0.0 copy-start.5
  0.1 0.6 copy-done.5
  0.7 0.0 copy-start.4
  0.8 0.7 copy-done.4
  1.4 0.1 constant_dynamic-slice_fusion
  1.5 0.1 copy.79
  1.6 0.1 stack.30
  1.7 0.1 compare_convert_fusion
  1.8 0.0 copy-start.3
  1.9 0.8 copy-done.3
  2.6 0.0 copy-start.1
  2.7 0.9 copy-done.1
  3.5 0.3 fusion.7
  3.8 0.3 fusion.6
  4.1 0.3 fusion.5
  4.4 0.3 fusion.4
  4.7 0.3 fusion.3
  5.1 0.3 fusion.2
  5.4 0.3 fusion.14
  5.7 4.1 %collective-permute-start = (f32[6,16,4]{1,0,2:T(8,128)S(1)}, f32[6,16,4]{1,0,2:T(8,128)S(1)}, u32[]{:S(2)}, u32[]{:S(2)}) collective-permute-start(f32[6,16,4]{1,0,2:T(8,128)S(1)} %get-tuple-element.16), channel_id=1, source_target_pairs={{0,16},{2,18},{4,20},{6,22},{8,24},{10,26},{12,28},{14,30},{16,0},... | collective-permute-start | bytes 4616 | tf_op jit(solution)/shard_map/ppermute | solution.py:15
  9.9 1.3 collective-permute-start.2
  11.1 0.0 collective-permute-start.6
  11.1 0.5 collective-permute-start.7
  11.6 1.5 %collective-permute-start.3 = (f32[6,16,4]{1,0,2:T(8,128)S(1)}, f32[6,16,4]{1,0,2:T(8,128)S(1)}, u32[]{:S(2)}, u32[]{:S(2)}) collective-permute-start(f32[6,16,4]{1,0,2:T(8,128)S(1)} %get-tuple-element.11), channel_id=1, source_target_pairs={{0,2},{2,4},{4,6},{6,8},{8,10},{10,12},{12,14},{14,16},{16,18},{18... | collective-permute-start | bytes 4616 | tf_op jit(solution)/shard_map/ppermute | solution.py:15
  13.1 0.0 collective-permute-done.6
  13.1 2.7 %collective-permute-start.1 = (f32[6,16,4]{1,0,2:T(8,128)S(1)}, f32[6,16,4]{1,0,2:T(8,128)S(1)}, u32[]{:S(2)}, u32[]{:S(2)}) collective-permute-start(f32[6,16,4]{1,0,2:T(8,128)S(1)} %get-tuple-element.15), channel_id=1, source_target_pairs={{0,16},{2,18},{4,20},{6,22},{8,24},{10,26},{12,28},{14,30},{16,0},... | collective-permute-start | bytes 4616 | tf_op jit(solution)/shard_map/ppermute | solution.py:15
  15.8 0.0 collective-permute-done.7
  15.8 2.1 %collective-permute-start.4 = (f32[6,16,4]{1,0,2:T(8,128)S(1)}, f32[6,16,4]{1,0,2:T(8,128)S(1)}, u32[]{:S(2)}, u32[]{:S(2)}) collective-permute-start(f32[6,16,4]{1,0,2:T(8,128)S(1)} %get-tuple-element.14), channel_id=1, source_target_pairs={{0,14},{2,16},{4,18},{6,20},{8,22},{10,24},{12,26},{14,28},{16,30}... | collective-permute-start | bytes 4616 | tf_op jit(solution)/shard_map/ppermute | solution.py:15
  17.9 0.0 collective-permute-done
  17.9 2.8 %collective-permute-start.5 = (f32[6,16,4]{1,0,2:T(8,128)S(1)}, f32[6,16,4]{1,0,2:T(8,128)S(1)}, u32[]{:S(2)}, u32[]{:S(2)}) collective-permute-start(f32[6,16,4]{1,0,2:T(8,128)S(1)} %get-tuple-element.14), channel_id=1, source_target_pairs={{0,30},{2,0},{4,2},{6,4},{8,6},{10,8},{12,10},{14,12},{16,14},{18,... | collective-permute-start | bytes 4616 | tf_op jit(solution)/shard_map/ppermute | solution.py:15
  20.7 0.1 copy.97
  20.8 0.0 copy-start.2
  20.8 0.1 reshape.403
  20.9 0.1 dynamic_slice.11
  21.0 0.0 collective-permute-done.1
  21.0 0.0 collective-permute-done.2
  21.0 0.0 collective-permute-done.3
  21.0 0.3 collective-permute-done.4
  21.3 0.8 collective-permute-done.5
  22.1 0.0 copy-done.2
  22.1 0.3 fusion.13
  22.4 1.8 %all_gather.6 = f32[6,16,8]{1,0,2:T(8,128)S(1)} all-gather(f32[6,16,4]{1,0,2:T(8,128)S(1)} %fusion.13), channel_id=1, replica_groups=mesh['sub'=16,'crs'=2] {'crs'}, dimensions={2}, use_global_device_ids=true | all-gather | bytes 4608 | tf_op jit(solution)/shard_map/all_gather | solution.py:85
  24.3 0.0 copy-done
  24.3 0.2 convolution_bitcast_fusion
  24.5 77.5 %psum.14 = f32[384,16]{0,1:T(8,128)S(1)} all-reduce(f32[384,16]{0,1:T(8,128)S(1)} %convolution_bitcast_fusion), channel_id=1, replica_groups=mesh['sub'=16,'crs'=2] {'sub'}, use_global_device_ids=true, to_apply=%region_1.2 | all-reduce | flops 6144 | bytes 49152 | tf_op jit(solution)/shard_map/psum | solution.py:88
  102.0 0.2 convolution_bitcast_fusion.8
  102.2 0.1 copy.94
  102.3 3.4 %psum.15 = f32[6,16,8]{1,0,2:T(8,128)S(1)} all-reduce(f32[6,16,8]{1,0,2:T(8,128)S(1)} %bitcast.135), channel_id=1, replica_groups=mesh['sub'=16,'crs'=2] {'crs'}, use_global_device_ids=true, to_apply=%region_2.3 | all-reduce | flops 768 | bytes 6144 | tf_op jit(solution)/shard_map/psum | solution.py:94
  105.7 37.6 %all_gather.7 = f32[6,16,128]{1,2,0:T(8,128)S(1)} all-gather(f32[6,16,8]{1,2,0:T(8,128)S(1)} %copy.96), channel_id=1, replica_groups=mesh['sub'=16,'crs'=2] {'sub'}, dimensions={2}, use_global_device_ids=true | all-gather | bytes 52224 | tf_op jit(solution)/shard_map/all_gather | solution.py:96
  143.3 0.3 fusion.44
  143.5 0.1 fusion.74
  143.6 0.4 fusion.35
  144.0 0.4 convolution_add_fusion.5
  144.3 0.4 convolution_add_fusion.4
  144.7 0.4 convolution_add_fusion.3
  145.0 0.4 convolution_add_fusion.2
  145.4 0.4 convolution_add_fusion.1
  145.8 0.4 fusion.1
  146.1 0.7 copy.112
  (22 shorter events, 0.2 us)
Async XLA Ops:
  0.0 24.3 %copy-start = (f32[48,384]{1,0:T(8,128)S(1)}, f32[48,384]{1,0:T(8,128)}, u32[]{:S(2)}) copy-start(f32[48,384]{1,0:T(8,128)} %param.11) | copy-start | bytes 221188
  0.0 0.7 copy-start.5
  0.7 0.7 copy-start.4
  1.8 0.8 copy-start.3
  2.6 0.9 copy-start.1
  5.7 12.2 %collective-permute-start = (f32[6,16,4]{1,0,2:T(8,128)S(1)}, f32[6,16,4]{1,0,2:T(8,128)S(1)}, u32[]{:S(2)}, u32[]{:S(2)}) collective-permute-start(f32[6,16,4]{1,0,2:T(8,128)S(1)} %get-tuple-element.16), channel_id=1, source_target_pairs={{0,16},{2,18},{4,20},{6,22},{8,24},{10,26},{12,28},{14,30},{16,0},... | collective-permute-start | bytes 4616 | tf_op jit(solution)/shard_map/ppermute | solution.py:15
  9.9 11.2 %collective-permute-start.2 = (f32[6,16,4]{1,0,2:T(8,128)S(1)}, f32[6,16,4]{1,0,2:T(8,128)S(1)}, u32[]{:S(2)}, u32[]{:S(2)}) collective-permute-start(f32[6,16,4]{1,0,2:T(8,128)S(1)} %get-tuple-element.11), channel_id=1, source_target_pairs={{0,18},{2,20},{4,22},{6,24},{8,26},{10,28},{12,30},{14,0},{16,2},{... | collective-permute-start | bytes 4616 | tf_op jit(solution)/shard_map/ppermute | solution.py:15
  11.1 2.0 %collective-permute-start.6 = (f32[6,16,1]{1,0,2:T(8,128)S(1)}, f32[6,16,1]{1,0,2:T(8,128)S(1)}, u32[]{:S(2)}, u32[]{:S(2)}) collective-permute-start(f32[6,16,1]{1,0,2:T(8,128)S(1)} %slice.71), channel_id=1, source_target_pairs={{0,1},{1,0},{2,3},{3,2},{4,5},{5,4},{6,7},{7,6},{8,9},{9,8},{10,11... | collective-permute-start | bytes 1160 | tf_op jit(solution)/shard_map/ppermute | solution.py:15
  11.1 4.7 %collective-permute-start.7 = (f32[6,16,1]{1,0,2:T(8,128)S(1)}, f32[6,16,1]{1,0,2:T(8,128)S(1)}, u32[]{:S(2)}, u32[]{:S(2)}) collective-permute-start(f32[6,16,1]{1,0,2:T(8,128)S(1)} %slice.75), channel_id=1, source_target_pairs={{0,1},{1,0},{2,3},{3,2},{4,5},{5,4},{6,7},{7,6},{8,9},{9,8},{10,11... | collective-permute-start | bytes 1160 | tf_op jit(solution)/shard_map/ppermute | solution.py:15
  11.6 9.4 %collective-permute-start.3 = (f32[6,16,4]{1,0,2:T(8,128)S(1)}, f32[6,16,4]{1,0,2:T(8,128)S(1)}, u32[]{:S(2)}, u32[]{:S(2)}) collective-permute-start(f32[6,16,4]{1,0,2:T(8,128)S(1)} %get-tuple-element.11), channel_id=1, source_target_pairs={{0,2},{2,4},{4,6},{6,8},{8,10},{10,12},{12,14},{14,16},{16,18},{18... | collective-permute-start | bytes 4616 | tf_op jit(solution)/shard_map/ppermute | solution.py:15
  13.1 7.9 %collective-permute-start.1 = (f32[6,16,4]{1,0,2:T(8,128)S(1)}, f32[6,16,4]{1,0,2:T(8,128)S(1)}, u32[]{:S(2)}, u32[]{:S(2)}) collective-permute-start(f32[6,16,4]{1,0,2:T(8,128)S(1)} %get-tuple-element.15), channel_id=1, source_target_pairs={{0,16},{2,18},{4,20},{6,22},{8,24},{10,26},{12,28},{14,30},{16,0},... | collective-permute-start | bytes 4616 | tf_op jit(solution)/shard_map/ppermute | solution.py:15
  15.8 5.5 %collective-permute-start.4 = (f32[6,16,4]{1,0,2:T(8,128)S(1)}, f32[6,16,4]{1,0,2:T(8,128)S(1)}, u32[]{:S(2)}, u32[]{:S(2)}) collective-permute-start(f32[6,16,4]{1,0,2:T(8,128)S(1)} %get-tuple-element.14), channel_id=1, source_target_pairs={{0,14},{2,16},{4,18},{6,20},{8,22},{10,24},{12,26},{14,28},{16,30}... | collective-permute-start | bytes 4616 | tf_op jit(solution)/shard_map/ppermute | solution.py:15
  17.9 4.2 %collective-permute-start.5 = (f32[6,16,4]{1,0,2:T(8,128)S(1)}, f32[6,16,4]{1,0,2:T(8,128)S(1)}, u32[]{:S(2)}, u32[]{:S(2)}) collective-permute-start(f32[6,16,4]{1,0,2:T(8,128)S(1)} %get-tuple-element.14), channel_id=1, source_target_pairs={{0,30},{2,0},{4,2},{6,4},{8,6},{10,8},{12,10},{14,12},{16,14},{18,... | collective-permute-start | bytes 4616 | tf_op jit(solution)/shard_map/ppermute | solution.py:15
  20.8 1.3 copy-start.2
where the time goes:
time: 147 us
  blocking collectives  120 us (82%)
  starting transfers between devices  14.9 us (10%)
  matrix products  5.56 us (4%)
  local copies, waits for them, and re-layouts  4.53 us (3%)
    psum x1, blocking collectives, body(): panel_rows = lax.psum(partial_rows, 'sub')  77.5 us
    all_gather x1, blocking collectives, body(): portion = lax.all_gather(group_amps, 'sub', axis=2, tiled=True)  37.6 us
    ppermute x8, starting transfers between devices, shifted(): lax.ppermute(value, axis, [(i, (i + by) % peers) for i in range(peers)])  14.9 us
    psum x1, blocking collectives, body(): group_amps = lax.psum(partial_modes, 'crs')  3.41 us
    unnamed x19, local copies, waits for them, and re-layouts  3.1 us
  transfers between devices with their start and end apart: 8, of which 2 were waited for; matrix products, arithmetic and copies ran while one was open for 0% of the time, Pallas kernels for 0%

commit v1 on v0

v1 whole, which is shorter than its diff:
```python
import jax
import jax.numpy as jnp
from jax import lax
from jax.sharding import PartitionSpec as P

MODES = 6
NFACE = 6
COL_LEN = 2
NDIR = 6
NBLOCK = 4

HIGHEST = lax.Precision.HIGHEST


def all_sum(value, axis):
    peers = lax.axis_size(axis)
    if peers & (peers - 1):
        return lax.psum(value, axis)
    step = 1
    while step < peers:
        value = value + lax.ppermute(value, axis, [(i, i ^ step) for i in range(peers)])
        step *= 2
    return value


def body(multipliers, own_modes, neighbour_modes, face_index, neighbour_list, coarse_factor):
    width_rhs, local_subs, _ = multipliers.shape
    crs_size = lax.axis_size("crs")
    sub_size = lax.axis_size("sub")
    crs_rank = lax.axis_index("crs")
    sub_rank = lax.axis_index("sub")
    group_subs = local_subs * crs_size
    row_len = sub_size // COL_LEN
    first_sub = (sub_rank * crs_size + crs_rank) * local_subs

    def ring(i, by):
        return i // row_len * row_len + (i + by) % row_len

    def fetched(source):
        return lax.ppermute(coarse_factor, "sub", [(source(i), i) for i in range(sub_size)])

    factors = [
        coarse_factor,
        fetched(lambda i: (i + row_len) % sub_size),
        fetched(lambda i: ring(i, 1)),
        fetched(lambda i: ring(i, -1)),
    ]

    local_ids = first_sub + lax.iota(jnp.int32, local_subs)
    first = local_ids // (row_len * group_subs)
    second = local_ids // group_subs % row_len
    third = local_ids % group_subs

    def place(a, b, c):
        return (a * row_len + b) * group_subs + c

    across = [
        place((first + 1) % COL_LEN, second, third),
        place(first, (second + 1) % row_len, third),
        place(first, (second + row_len - 1) % row_len, third),
        place(first, second, (third + 1) % group_subs),
        place(first, second, (third + group_subs - 1) % group_subs),
    ]
    local_nbrs = lax.dynamic_slice_in_dim(neighbour_list, first_sub, local_subs, 0)
    face_dir = jnp.zeros_like(local_nbrs)
    for which in range(NDIR - 2, -1, -1):
        face_dir = jnp.where(local_nbrs == across[which][:, None], which + 1, face_dir)
    point_dir = jnp.zeros_like(face_index)
    for which_face in range(NFACE):
        point_dir = jnp.where(
            face_index == which_face, face_dir[:, which_face : which_face + 1], point_dir
        )
    rows = [own_modes]
    for which in range(1, NDIR):
        rows.append(jnp.where((point_dir == which)[None], neighbour_modes, 0.0))
    rows = jnp.stack(rows)
    sums = jnp.einsum("dksm,rsm->rsdk", rows, multipliers, precision=HIGHEST)

    blocks = jnp.array([0, 1, 2, 3, 0, 0], jnp.int32)
    moves = jnp.array([0, 0, 0, 0, 1, group_subs - 1], jnp.int32)
    target_sub = (third[:, None] + moves[None]) % group_subs
    target = (blocks[None] * group_subs + target_sub)[:, :, None] * MODES + lax.iota(jnp.int32, MODES)
    wide = NBLOCK * group_subs * MODES
    chosen = (target.reshape(-1, 1) == lax.iota(jnp.int32, wide)[None]).astype(jnp.float32)

    coarse = jnp.dot(sums.reshape(width_rhs, -1), chosen, precision=HIGHEST)
    coarse = all_sum(coarse, "crs").reshape(width_rhs, NBLOCK, group_subs * MODES)
    panel = 0.0
    for which in range(NBLOCK):
        panel = panel + jnp.dot(coarse[:, which], factors[which], precision=HIGHEST)
    panel = all_sum(panel, "sub")
    amps = jnp.concatenate(
        [jnp.einsum("rp,cp->rc", panel, f, precision=HIGHEST) for f in factors], axis=1
    )
    amps = all_sum(amps, "crs")
    near = jnp.einsum("rw,nw->rn", amps, chosen, precision=HIGHEST)
    near = near.reshape(width_rhs, local_subs, NDIR, MODES)
    return multipliers - jnp.einsum("rsdk,dksm->rsm", near, rows, precision=HIGHEST)


def solution(mesh):
    placed = (
        P(None, ("sub", "crs"), None),
        P(None, ("sub", "crs"), None),
        P(None, ("sub", "crs"), None),
        P(("sub", "crs"), None),
        P(),
        P("sub", "crs"),
    )
    return jax.shard_map(
        body, mesh=mesh, in_specs=placed, out_specs=P(None, ("sub", "crs"), None), check_vma=False
    )
```

time: 147 us -> 36.8 us (0.25)
  blocking collectives: 120 us -> 0 us
  waiting for transfers between devices: 1.11 us -> 13.9 us
  matrix products: 5.56 us -> 2.88 us
    psum x2 -> x0, blocking collectives: 80.9 us -> none  [the longest x1 77.5 us: body(): panel_rows = lax.psum(partial_rows, 'sub')]
    all_gather x2 -> x0, blocking collectives: 39.4 us -> none  [the longest x1 37.6 us: body(): portion = lax.all_gather(group_amps, 'sub', axis=2, tiled=True)]
    ppermute x8 -> x9, waiting for transfers between devices: 1.11 us -> 13.9 us  [the longest x6 11.6 us: all_sum(): lax.ppermute(value, axis, [(i, i ^ step) for i in range(peers)])]
    dot_general x18 -> x12, matrix products: 5.56 us -> 2.88 us  [the longest x4 0.75 us: body(): jnp.einsum('rp,cp->rc', panel, f, precision=HIGHEST)]
    ppermute x8 -> x9, starting transfers between devices: 14.9 us -> 14.2 us  [the longest x3 7.48 us: fetched(): lax.ppermute(coarse_factor, 'sub', [(source(i), i) for i in range(sub_siz...]
    unnamed x19 -> x17, local copies, waits for them, and re-layouts: 3.1 us -> 3.55 us
  transfers between devices with their start and end apart: 8 -> 9, of which waited for: 2 -> 8; matrix products, arithmetic and copies ran while one was open for 0% -> 2% of each run, Pallas kernels for 0% -> 0%
where the time goes in v1:
time: 36.8 us; the launch traced here: 36.5 us
  starting transfers between devices  14.2 us (39%)
  waiting for transfers between devices  13.9 us (38%)
  local copies, waits for them, and re-layouts  4.62 us (13%)
  matrix products  2.88 us (8%)
  other arithmetic  0.63 us (2%)
    ppermute x6, waiting for transfers between devices, all_sum(): lax.ppermute(value, axis, [(i, i ^ step) for i in range(peers)])  11.6 us
    ppermute x3, starting transfers between devices, fetched(): lax.ppermute(coarse_factor, 'sub', [(source(i), i) for i in range(sub_siz...  7.48 us
    ppermute x6, starting transfers between devices, all_sum(): lax.ppermute(value, axis, [(i, i ^ step) for i in range(peers)])  6.71 us
    unnamed x17, local copies, waits for them, and re-layouts  3.55 us
    ppermute x3, waiting for transfers between devices, fetched(): lax.ppermute(coarse_factor, 'sub', [(source(i), i) for i in range(sub_siz...  2.39 us
    dot_general x4, matrix products, body(): jnp.einsum('rp,cp->rc', panel, f, precision=HIGHEST)  0.75 us
    sub x1, local copies, waits for them, and re-layouts, body(): multipliers - jnp.einsum('rsdk,dksm->rsm', near, rows, precision=HIGHEST)  0.74 us
  transfers between devices with their start and end apart: 9, of which 8 were waited for; matrix products, arithmetic and copies ran while one was open for 2% of the time, Pallas kernels for 0%

profile of v1, /device:TPU:0, one launch (start us, length us, event | category | flops | bytes accessed | tf_op | source)
XLA Modules:
  0.0 36.5 jit_solution(3473194074240114128)
XLA Ops:
  0.0 0.0 copy-start.5
  0.0 0.0 copy-start.3
  0.1 0.6 %copy-done.5 = s32[128,6]{0,1:T(8,128)S(1)} copy-done((s32[128,6]{0,1:T(8,128)S(1)}, s32[128,6]{0,1:T(8,128)}, u32[]{:S(2)}) %copy-start.5) | copy-done | bytes 3096
  0.7 0.1 select_select_fusion.1
  0.8 0.0 copy-start.4
  0.8 0.7 %copy-done.4 = s32[4,512]{1,0:T(4,128)S(1)} copy-done((s32[4,512]{1,0:T(4,128)S(1)}, s32[4,512]{1,0:T(4,128)}, u32[]{:S(2)}) %copy-start.4) | copy-done | bytes 8216
  1.5 0.1 broadcast_compare_fusion.4
  1.6 0.0 copy-done.3
  1.6 0.0 copy-start
  1.6 0.8 %copy-done = f32[6,4,512]{2,1,0:T(4,128)S(1)} copy-done((f32[6,4,512]{2,1,0:T(4,128)S(1)}, f32[6,4,512]{2,1,0:T(4,128)}, u32[]{:S(2)}) %copy-start) | copy-done | bytes 49176
  2.5 0.0 copy-start.1
  2.5 0.8 %copy-done.1 = f32[16,4,512]{2,1,0:T(4,128)S(1)} copy-done((f32[16,4,512]{2,1,0:T(4,128)S(1)}, f32[16,4,512]{2,1,0:T(4,128)}, u32[]{:S(2)}) %copy-start.1) | copy-done | bytes 131096
  3.4 0.5 %convolution_bitcast_fusion.1 = f32[16,4,6,6]{0,3,2,1:T(8,128)S(1)} fusion(f32[6,6,4,512]{3,1,0,2:T(8,128)S(1)} %fusion.16, f32[16,4,512,1]{2,1,0,3:T(4,128)S(1)} %bitcast.80), kind=kOutput, calls=%fused_computation.2 | convolution fusion | flops 14155776 | bytes 435200 | tf_op jit(solution)/shard_map/dksm,rsm->rsdk/dot_general | solution.py:77
  3.9 0.0 copy-start.6
  3.9 0.0 copy-start.7
  4.0 0.0 copy-start.2
  4.0 0.6 %copy-done.6 = s32[6]{0:T(128)S(1)} copy-done((s32[6]{0:T(128)S(1)}, s32[6]{0:T(128)}, u32[]{:S(2)}) %copy-start.6) | copy-done | bytes 48
  4.6 0.0 copy-done.7
  4.6 0.1 fusion.19
  4.7 0.1 copy.35
  4.8 0.1 iota_add_fusion
  4.9 0.1 add.374
  5.0 0.3 fusion.3
  5.2 0.5 %collective-permute-start = (f32[16,192]{1,0:T(8,128)S(1)}, f32[16,192]{1,0:T(8,128)S(1)}, u32[]{:S(2)}, u32[]{:S(2)}) collective-permute-start(f32[16,192]{1,0:T(8,128)S(1)} %fusion.3), channel_id=1, source_target_pairs={{0,1},{1,0},{2,3},{3,2},{4,5},{5,4},{6,7},{7,6},{8,9},{9,8},{10,11... | collective-permute-start | bytes 36872 | tf_op jit(solution)/shard_map/ppermute | solution.py:21
  5.7 0.0 copy-done.2
  5.7 3.7 %collective-permute-start.1 = (f32[48,384]{1,0:T(8,128)S(1)}, f32[48,384]{1,0:T(8,128)S(1)}, u32[]{:S(2)}, u32[]{:S(2)}) collective-permute-start(f32[48,384]{1,0:T(8,128)S(1)} %copy-done.2), channel_id=1, source_target_pairs={{16,0},{18,2},{20,4},{22,6},{24,8},{26,10},{28,12},{30,14},{0,16},... | collective-permute-start | bytes 221192 | tf_op jit(solution)/shard_map/ppermute | solution.py:40
  9.4 1.5 %collective-permute-start.3 = (f32[48,384]{1,0:T(8,128)S(1)}, f32[48,384]{1,0:T(8,128)S(1)}, u32[]{:S(2)}, u32[]{:S(2)}) collective-permute-start(f32[48,384]{1,0:T(8,128)S(1)} %copy-done.2), channel_id=1, source_target_pairs={{14,0},{0,2},{2,4},{4,6},{6,8},{8,10},{10,12},{12,14},{30,16},{16,... | collective-permute-start | bytes 221192 | tf_op jit(solution)/shard_map/ppermute | solution.py:40
  10.9 2.3 %collective-permute-start.2 = (f32[48,384]{1,0:T(8,128)S(1)}, f32[48,384]{1,0:T(8,128)S(1)}, u32[]{:S(2)}, u32[]{:S(2)}) collective-permute-start(f32[48,384]{1,0:T(8,128)S(1)} %copy-done.2), channel_id=1, source_target_pairs={{2,0},{4,2},{6,4},{8,6},{10,8},{12,10},{14,12},{0,14},{18,16},{20,... | collective-permute-start | bytes 221192 | tf_op jit(solution)/shard_map/ppermute | solution.py:40
  13.2 0.0 collective-permute-done
  13.2 0.1 reshape.218
  13.4 0.5 %collective-permute-done.1 = f32[48,384]{1,0:T(8,128)S(1)} collective-permute-done((f32[48,384]{1,0:T(8,128)S(1)}, f32[48,384]{1,0:T(8,128)S(1)}, u32[]{:S(2)}, u32[]{:S(2)}) %collective-permute-start.1) | collective-permute-done | bytes 73760 | tf_op jit(solution)/shard_map/ppermute | solution.py:40
  13.8 0.2 fusion.36
  14.0 0.2 convolution_add_fusion.1
  14.2 1.8 %collective-permute-done.3 = f32[48,384]{1,0:T(8,128)S(1)} collective-permute-done((f32[48,384]{1,0:T(8,128)S(1)}, f32[48,384]{1,0:T(8,128)S(1)}, u32[]{:S(2)}, u32[]{:S(2)}) %collective-permute-start.3) | collective-permute-done | bytes 73760 | tf_op jit(solution)/shard_map/ppermute | solution.py:40
  16.0 0.2 fusion.37
  16.2 0.1 collective-permute-done.2
  16.3 0.2 fusion.1
  16.4 1.6 %collective-permute-start.4 = (f32[16,384]{1,0:T(8,128)S(1)}, f32[16,384]{1,0:T(8,128)S(1)}, u32[]{:S(2)}, u32[]{:S(2)}) collective-permute-start(f32[16,384]{1,0:T(8,128)S(1)} %fusion.1), channel_id=1, source_target_pairs={{0,2},{2,0},{4,6},{6,4},{8,10},{10,8},{12,14},{14,12},{16,18},{18,... | collective-permute-start | bytes 73736 | tf_op jit(solution)/shard_map/ppermute | solution.py:21
  18.0 2.3 %collective-permute-done.4 = f32[16,384]{1,0:T(8,128)S(1)} collective-permute-done((f32[16,384]{1,0:T(8,128)S(1)}, f32[16,384]{1,0:T(8,128)S(1)}, u32[]{:S(2)}, u32[]{:S(2)}) %collective-permute-start.4) | collective-permute-done | bytes 24608 | tf_op jit(solution)/shard_map/ppermute | solution.py:21
  20.3 1.8 %collective-permute-start.5 = (f32[16,384]{1,0:T(8,128)S(1)}, f32[16,384]{1,0:T(8,128)S(1)}, u32[]{:S(2)}, u32[]{:S(2)}) collective-permute-start(f32[16,384]{1,0:T(8,128)S(1)} %add.379), channel_id=1, source_target_pairs={{0,4},{2,6},{4,0},{6,2},{8,12},{10,14},{12,8},{14,10},{16,20},{18,... | collective-permute-start | bytes 73736 | tf_op jit(solution)/shard_map/ppermute | solution.py:21
  22.1 2.0 %collective-permute-done.5 = f32[16,384]{1,0:T(8,128)S(1)} collective-permute-done((f32[16,384]{1,0:T(8,128)S(1)}, f32[16,384]{1,0:T(8,128)S(1)}, u32[]{:S(2)}, u32[]{:S(2)}) %collective-permute-start.5) | collective-permute-done | bytes 24608 | tf_op jit(solution)/shard_map/ppermute | solution.py:21
  24.2 1.6 %collective-permute-start.6 = (f32[16,384]{1,0:T(8,128)S(1)}, f32[16,384]{1,0:T(8,128)S(1)}, u32[]{:S(2)}, u32[]{:S(2)}) collective-permute-start(f32[16,384]{1,0:T(8,128)S(1)} %add.380), channel_id=1, source_target_pairs={{0,8},{2,10},{4,12},{6,14},{8,0},{10,2},{12,4},{14,6},{16,24},{18,... | collective-permute-start | bytes 73736 | tf_op jit(solution)/shard_map/ppermute | solution.py:21
  25.7 2.5 %collective-permute-done.6 = f32[16,384]{1,0:T(8,128)S(1)} collective-permute-done((f32[16,384]{1,0:T(8,128)S(1)}, f32[16,384]{1,0:T(8,128)S(1)}, u32[]{:S(2)}, u32[]{:S(2)}) %collective-permute-start.6) | collective-permute-done | bytes 24608 | tf_op jit(solution)/shard_map/ppermute | solution.py:21
  28.3 1.2 %collective-permute-start.7 = (f32[16,384]{1,0:T(8,128)S(1)}, f32[16,384]{1,0:T(8,128)S(1)}, u32[]{:S(2)}, u32[]{:S(2)}) collective-permute-start(f32[16,384]{1,0:T(8,128)S(1)} %add.381), channel_id=1, source_target_pairs={{0,16},{2,18},{4,20},{6,22},{8,24},{10,26},{12,28},{14,30},{16,0},... | collective-permute-start | bytes 73736 | tf_op jit(solution)/shard_map/ppermute | solution.py:21
  29.5 3.5 %collective-permute-done.7 = f32[16,384]{1,0:T(8,128)S(1)} collective-permute-done((f32[16,384]{1,0:T(8,128)S(1)}, f32[16,384]{1,0:T(8,128)S(1)}, u32[]{:S(2)}, u32[]{:S(2)}) %collective-permute-start.7) | collective-permute-done | bytes 24608 | tf_op jit(solution)/shard_map/ppermute | solution.py:21
  33.0 0.2 fusion.38
  33.2 0.2 fusion.39
  33.4 0.2 fusion.40
  33.6 0.2 fusion.41
  33.8 0.1 pad_maximum_fusion
  33.8 0.0 collective-permute-start.8
  33.9 1.2 %collective-permute-done.8 = f32[16,192]{1,0:T(8,128)S(1)} collective-permute-done((f32[16,192]{1,0:T(8,128)S(1)}, f32[16,192]{1,0:T(8,128)S(1)}, u32[]{:S(2)}, u32[]{:S(2)}) %collective-permute-start.8) | collective-permute-done | bytes 12320 | tf_op jit(solution)/shard_map/ppermute | solution.py:21
  35.0 0.3 fusion.2
  35.3 0.4 %fusion = f32[16,4,512]{2,0,1:T(8,128)S(1)} fusion(f32[6,6,4,512]{3,1,0,2:T(8,128)S(1)} %fusion.16, f32[16,4,6,6]{0,3,2,1:T(8,128)S(1)} %reshape.219, f32[16,4,512]{2,1,0:T(4,128)S(1)} %copy-done.1), kind=kOutput, calls=%fused_computation.1 | convolution fusion | flops 14188544 | bytes 566272 | tf_op jit(solution)/shard_map/rsdk,dksm->rsm/dot_general | solution.py:98
  35.7 0.7 %copy.38 = f32[16,4,512]{2,1,0:T(4,128)} copy(f32[16,4,512]{2,0,1:T(8,128)S(1)} %fusion) | data formatting | bytes 262144 | tf_op jit(solution)/shard_map/sub | solution.py:98
  (19 shorter events, 0.3 us)
Async XLA Ops:
  0.0 0.7 %copy-start.5 = (s32[128,6]{0,1:T(8,128)S(1)}, s32[128,6]{0,1:T(8,128)}, u32[]{:S(2)}) copy-start(s32[128,6]{0,1:T(8,128)} %param.12) | copy-start | bytes 9220
  0.0 1.6 %copy-start.3 = (f32[6,4,512]{2,1,0:T(4,128)S(1)}, f32[6,4,512]{2,1,0:T(4,128)}, u32[]{:S(2)}) copy-start(f32[6,4,512]{2,1,0:T(4,128)} %param.9) | copy-start | bytes 147460
  0.8 0.7 %copy-start.4 = (s32[4,512]{1,0:T(4,128)S(1)}, s32[4,512]{1,0:T(4,128)}, u32[]{:S(2)}) copy-start(s32[4,512]{1,0:T(4,128)} %param.11) | copy-start | bytes 24580
  1.6 0.8 %copy-start = (f32[6,4,512]{2,1,0:T(4,128)S(1)}, f32[6,4,512]{2,1,0:T(4,128)}, u32[]{:S(2)}) copy-start(f32[6,4,512]{2,1,0:T(4,128)} %param.10) | copy-start | bytes 147460
  2.5 0.9 %copy-start.1 = (f32[16,4,512]{2,1,0:T(4,128)S(1)}, f32[16,4,512]{2,1,0:T(4,128)}, u32[]{:S(2)}) copy-start(f32[16,4,512]{2,1,0:T(4,128)} %param.8) | copy-start | bytes 393220
  3.9 0.7 %copy-start.6 = (s32[6]{0:T(128)S(1)}, s32[6]{0:T(128)}, u32[]{:S(2)}) copy-start(s32[6]{0:T(128)} %constant.121.clone) | copy-start | bytes 76
  3.9 0.7 %copy-start.7 = (s32[6]{0:T(128)S(1)}, s32[6]{0:T(128)}, u32[]{:S(2)}) copy-start(s32[6]{0:T(128)} %constant.126) | copy-start | bytes 76
  4.0 1.8 %copy-start.2 = (f32[48,384]{1,0:T(8,128)S(1)}, f32[48,384]{1,0:T(8,128)}, u32[]{:S(2)}) copy-start(f32[48,384]{1,0:T(8,128)} %param.13) | copy-start | bytes 221188
  5.2 8.0 %collective-permute-start = (f32[16,192]{1,0:T(8,128)S(1)}, f32[16,192]{1,0:T(8,128)S(1)}, u32[]{:S(2)}, u32[]{:S(2)}) collective-permute-start(f32[16,192]{1,0:T(8,128)S(1)} %fusion.3), channel_id=1, source_target_pairs={{0,1},{1,0},{2,3},{3,2},{4,5},{5,4},{6,7},{7,6},{8,9},{9,8},{10,11... | collective-permute-start | bytes 36872 | tf_op jit(solution)/shard_map/ppermute | solution.py:21
  5.7 8.1 %collective-permute-start.1 = (f32[48,384]{1,0:T(8,128)S(1)}, f32[48,384]{1,0:T(8,128)S(1)}, u32[]{:S(2)}, u32[]{:S(2)}) collective-permute-start(f32[48,384]{1,0:T(8,128)S(1)} %copy-done.2), channel_id=1, source_target_pairs={{16,0},{18,2},{20,4},{22,6},{24,8},{26,10},{28,12},{30,14},{0,16},... | collective-permute-start | bytes 221192 | tf_op jit(solution)/shard_map/ppermute | solution.py:40
  9.4 6.6 %collective-permute-start.3 = (f32[48,384]{1,0:T(8,128)S(1)}, f32[48,384]{1,0:T(8,128)S(1)}, u32[]{:S(2)}, u32[]{:S(2)}) collective-permute-start(f32[48,384]{1,0:T(8,128)S(1)} %copy-done.2), channel_id=1, source_target_pairs={{14,0},{0,2},{2,4},{4,6},{6,8},{8,10},{10,12},{12,14},{30,16},{16,... | collective-permute-start | bytes 221192 | tf_op jit(solution)/shard_map/ppermute | solution.py:40
  10.9 5.4 %collective-permute-start.2 = (f32[48,384]{1,0:T(8,128)S(1)}, f32[48,384]{1,0:T(8,128)S(1)}, u32[]{:S(2)}, u32[]{:S(2)}) collective-permute-start(f32[48,384]{1,0:T(8,128)S(1)} %copy-done.2), channel_id=1, source_target_pairs={{2,0},{4,2},{6,4},{8,6},{10,8},{12,10},{14,12},{0,14},{18,16},{20,... | collective-permute-start | bytes 221192 | tf_op jit(solution)/shard_map/ppermute | solution.py:40
  16.4 3.9 %collective-permute-start.4 = (f32[16,384]{1,0:T(8,128)S(1)}, f32[16,384]{1,0:T(8,128)S(1)}, u32[]{:S(2)}, u32[]{:S(2)}) collective-permute-start(f32[16,384]{1,0:T(8,128)S(1)} %fusion.1), channel_id=1, source_target_pairs={{0,2},{2,0},{4,6},{6,4},{8,10},{10,8},{12,14},{14,12},{16,18},{18,... | collective-permute-start | bytes 73736 | tf_op jit(solution)/shard_map/ppermute | solution.py:21
  20.3 3.8 %collective-permute-start.5 = (f32[16,384]{1,0:T(8,128)S(1)}, f32[16,384]{1,0:T(8,128)S(1)}, u32[]{:S(2)}, u32[]{:S(2)}) collective-permute-start(f32[16,384]{1,0:T(8,128)S(1)} %add.379), channel_id=1, source_target_pairs={{0,4},{2,6},{4,0},{6,2},{8,12},{10,14},{12,8},{14,10},{16,20},{18,... | collective-permute-start | bytes 73736 | tf_op jit(solution)/shard_map/ppermute | solution.py:21
  24.2 4.1 %collective-permute-start.6 = (f32[16,384]{1,0:T(8,128)S(1)}, f32[16,384]{1,0:T(8,128)S(1)}, u32[]{:S(2)}, u32[]{:S(2)}) collective-permute-start(f32[16,384]{1,0:T(8,128)S(1)} %add.380), channel_id=1, source_target_pairs={{0,8},{2,10},{4,12},{6,14},{8,0},{10,2},{12,4},{14,6},{16,24},{18,... | collective-permute-start | bytes 73736 | tf_op jit(solution)/shard_map/ppermute | solution.py:21
  28.3 4.7 %collective-permute-start.7 = (f32[16,384]{1,0:T(8,128)S(1)}, f32[16,384]{1,0:T(8,128)S(1)}, u32[]{:S(2)}, u32[]{:S(2)}) collective-permute-start(f32[16,384]{1,0:T(8,128)S(1)} %add.381), channel_id=1, source_target_pairs={{0,16},{2,18},{4,20},{6,22},{8,24},{10,26},{12,28},{14,30},{16,0},... | collective-permute-start | bytes 73736 | tf_op jit(solution)/shard_map/ppermute | solution.py:21
  33.8 1.2 %collective-permute-start.8 = (f32[16,192]{1,0:T(8,128)S(1)}, f32[16,192]{1,0:T(8,128)S(1)}, u32[]{:S(2)}, u32[]{:S(2)}) collective-permute-start(f32[16,192]{1,0:T(8,128)S(1)} %pad_maximum_fusion), channel_id=1, source_target_pairs={{0,1},{1,0},{2,3},{3,2},{4,5},{5,4},{6,7},{7,6},{8,9},{9,8},{10,11... | collective-permute-start | bytes 36872 | tf_op jit(solution)/shard_map/ppermute | solution.py:21
